TPU v7x, 32 devices: a whole 2x2x4 slice. The times are simulated.
32 devices in a mesh: rows: 8 (over z, x), cols: 4 (over y, core).
Axes of the slice: x: 2, y: 2, z: 4, core: 2. Of those that a mesh axis runs over, the one named last changes fastest.
Arguments:
- grad_out: bfloat16 [32, 512, 192], P(('rows', 'cols')), may hold values from -6 to 6
- inputs: bfloat16 [64, 1024, 192], P('rows', 'cols'), may hold values from -6 to 6
- weight: bfloat16 [3, 3, 192, 192], replicated, may hold values from -0.15625 to 0.15625
Outputs:
- input_grad: bfloat16 [64, 1024, 192], P('rows', 'cols')
- filter_grad: float32 [3, 3, 192, 192], replicated
All inputs are finite; a program needn't handle non-finite values.
Results may differ from a plain program's by a relative error of at most 0.0028.
Values may be sent and summed in bfloat16 or wider, within the bound.
A program may use at most 64 MiB of HBM per device.

v0:
```python
import math
import jax
import jax.numpy as jnp
from jax import lax
from jax.sharding import PartitionSpec as P


def shifted(x, axis, by):
    devices = lax.axis_size(axis)
    pairs = [(i, i + by) for i in range(devices) if 0 <= i + by < devices]
    return lax.ppermute(x, axis, pairs)


def tap_products(out_block, flat_weight):
    chans = flat_weight.shape[0]
    flat = out_block.reshape(-1, chans)
    products = jnp.dot(flat, flat_weight, preferred_element_type=jnp.float32)
    return products.reshape(out_block.shape[0], out_block.shape[1], 3, 3, chans)


def assemble(products, count_rows, count_cols):
    rows_even = products[:count_rows, :, 1]
    rows_odd = products[:count_rows, :, 2] + products[1 : count_rows + 1, :, 0]

    def columns(mixed):
        even = mixed[:, :count_cols, 1]
        odd = mixed[:, :count_cols, 2] + mixed[:, 1 : count_cols + 1, 0]
        return jnp.stack([even, odd], axis=2)

    placed = jnp.stack([columns(rows_even), columns(rows_odd)], axis=1)
    return placed.reshape(2 * count_rows, 2 * count_cols, products.shape[-1])


def filter_terms(input_band, out_band, row_taps):
    count_rows, count_cols, chans = out_band.shape
    split = input_band.reshape(count_rows + 1, 2, count_cols + 1, 2, chans)
    offsets = ((0, 0), (0, 1), (1, 0))
    pieces = []
    for row_tap in row_taps:
        start_row, parity_row = offsets[row_tap]
        for col_tap in range(3):
            start_col, parity_col = offsets[col_tap]
            pieces.append(
                split[
                    start_row : start_row + count_rows,
                    parity_row,
                    start_col : start_col + count_cols,
                    parity_col,
                ]
            )
    stacked = jnp.stack(pieces, axis=2).reshape(count_rows * count_cols, len(pieces) * chans)
    flat_out = out_band.reshape(count_rows * count_cols, chans)
    return lax.dot_general(
        stacked, flat_out, (((0,), (0,)), ((), ())), preferred_element_type=jnp.float32
    )


def per_device(grad_out, inputs, weight):
    chans = weight.shape[2]
    rows_local, cols_local = (inputs.shape[0], inputs.shape[1])
    half_rows, half_cols = (rows_local // 2, cols_local // 2)
    whole = lax.all_gather(grad_out, "cols", axis=0, tiled=True)
    out_grad = lax.dynamic_slice_in_dim(whole, lax.axis_index("cols") * half_cols, half_cols, 1)
    flat_weight = jnp.transpose(weight, (3, 0, 1, 2)).reshape(chans, 9 * chans)
    above = shifted(inputs[-1:], "rows", 1)
    with_above = jnp.concatenate([above, inputs], axis=0)
    left = shifted(with_above[:, -1:], "cols", 1)
    input_band = jnp.pad(jnp.concatenate([left, with_above], axis=1), ((0, 1), (0, 1), (0, 0)))
    positions = half_rows * lax.axis_size("rows") * (half_cols * lax.axis_size("cols"))
    scale = 1.0 / math.sqrt(positions)
    buckets = []
    for row_tap in range(3):
        terms = filter_terms(input_band, out_grad, (row_tap,))
        buckets.append(lax.psum(terms, ("rows", "cols")))
    summed = jnp.concatenate(buckets, axis=0)
    filter_grad = summed.reshape(3, 3, chans, chans) * scale
    framed = jnp.pad(out_grad, ((1, 1), (1, 1), (0, 0)))
    placed = assemble(tap_products(framed, flat_weight), half_rows + 1, half_cols + 1)
    extended = placed[1:, 1:]
    below = shifted(extended[:1].astype(jnp.bfloat16), "rows", -1).astype(jnp.float32)
    own_rows = extended[1:].at[-1].add(below[0])
    right = shifted(own_rows[:, :1], "cols", -1)
    input_grad = own_rows[:, 1:].at[:, -1].add(right[:, 0])
    return (input_grad.astype(jnp.bfloat16), filter_grad)


def solution(mesh):
    in_specs = (P(("rows", "cols"), None, None), P("rows", "cols", None), P())
    out_specs = (P("rows", "cols", None), P())
    return jax.shard_map(
        per_device, mesh=mesh, in_specs=in_specs, out_specs=out_specs, check_vma=False
    )
```

profile of v0, /device:TPU:0, one launch (start us, length us, event | category | flops | bytes accessed | tf_op | source)
XLA Modules:
  0.0 208.3 jit_solution(10896684272660905231)
XLA Ops:
  7.2 1.0 slice.137
  8.2 4.9 %collective-permute-start.2 = (bf16[1,256,192]{1,2,0:T(8,128)(2,1)S(1)}, bf16[1,256,192]{1,2,0:T(8,128)(2,1)S(1)}, u32[]{:S(2)}, u32[]{:S(2)}) collective-permute-start(bf16[1,256,192]{1,2,0:T(8,128)(2,1)S(1)} %slice.137), channel_id=1, source_target_pairs={{0,4},{4,8},{8,12},{12,16},{16,20},{20,24},{24,28},{1,5},{5,9},{9,... | collective-permute-start | bytes 294920 | tf_op jit(solution)/shard_map/ppermute | solution.py:11
  13.1 8.8 %all_gather.3 = bf16[4,512,192]{1,2,0:T(8,128)(2,1)S(1)} all-gather(bf16[1,512,192]{1,2,0:T(8,128)(2,1)} %param.7), channel_id=1, replica_groups=mesh['rows'=8,'cols'=4] {'cols'}, dimensions={0}, use_global_device_ids=true | all-gather | bytes 983040 | tf_op jit(solution)/shard_map/all_gather | solution.py:62
  21.9 0.1 copy.90
  22.1 1.2 fusion.1
  23.3 0.4 slice_bitcast_fusion
  23.7 0.4 fusion.16
  24.2 1.2 maximum_bitcast_fusion.1
  25.5 0.2 slice.163
  25.7 2.5 %collective-permute-start.3 = (bf16[9,1,192]{1,2,0:T(8,128)(2,1)S(1)}, bf16[9,1,192]{1,2,0:T(8,128)(2,1)S(1)}, u32[]{:S(2)}, u32[]{:S(2)}) collective-permute-start(bf16[9,1,192]{1,2,0:T(8,128)(2,1)S(1)} %slice.163), channel_id=1, source_target_pairs={{0,1},{1,2},{2,3},{4,5},{5,6},{6,7},{8,9},{9,10},{10,11},{12,13},{... | collective-permute-start | bytes 10376 | tf_op jit(solution)/shard_map/ppermute | solution.py:11
  28.2 1.3 maximum_bitcast_fusion
  29.4 0.7 pad_maximum_fusion.1
  30.1 1.7 copy.92
  31.8 2.6 %pad.13.clone = bf16[10,258,192]{2,1,0:T(8,128)(2,1)} pad(bf16[9,257,192]{2,1,0:T(8,128)(2,1)} %copy.92, bf16[]{:T(256)} %constant.66.clone.1), padding=0_1x0_1x0_0 | pad | bytes 1878914 | tf_op jit(solution)/shard_map/jit(_pad)/pad | solution.py:68
  34.3 3.1 %reshape.97 = bf16[5,2,129,2,192]{4,3,2,1,0:T(2,128)(2,1)S(1)} reshape(bf16[10,258,192]{2,1,0:T(8,128)(2,1)} %pad.13.clone) | data formatting | bytes 1981440 | tf_op jit(solution)/shard_map/reshape | solution.py:36
  37.5 4.5 %fusion.18 = (bf16[4,1,128,1,192]{4,3,2,1,0:T(2,128)(2,1)S(1)}, bf16[4,1,128,1,192]{4,3,2,1,0:T(2,128)(2,1)}, bf16[4,1,128,1,192]{4,3,2,1,0:T(2,128)(2,1)S(1)}, ...) fusion(bf16[5,2,129,2,192]{4,3,2,1,0:T(2,128)(2,1)S(1)} %reshape.97), kind=kLoop, calls=%fused_computation.36 | loop fusion | bytes 3538944 | tf_op jit(solution)/shard_map/slice | solution.py:44
  41.9 1.2 copy.77
  43.2 1.2 copy.76
  44.4 1.3 copy.75
  45.8 0.5 copy.78
  46.3 1.2 copy.81
  47.5 1.9 copy.80
  49.4 0.9 copy.79
  50.3 1.1 pad_maximum_fusion.3
  51.4 0.5 copy.82
  51.9 1.2 fusion.9
  53.1 1.2 fusion.6
  54.2 0.3 copy.85
  54.6 0.4 copy.84
  55.0 0.4 copy.83
  55.4 0.5 copy.86
  55.9 1.2 fusion.3
  57.1 1.5 pad_maximum_fusion
  58.6 1.4 copy.73
  60.0 2.9 %reshape.96 = f32[10,258,192]{2,1,0:T(8,128)} reshape(f32[5,2,129,2,192]{4,3,2,1,0:T(2,128)S(1)} %copy.73) | data formatting | bytes 3962880 | tf_op jit(solution)/shard_map/reshape | solution.py:31
  62.9 1.0 slice.187
  63.9 1.3 collective-permute-start
  65.2 1.8 slice.157
  67.0 4.9 %collective-permute-done = bf16[1,257,192]{2,1,0:T(8,128)(2,1)S(1)} collective-permute-done((bf16[1,257,192]{2,1,0:T(8,128)(2,1)S(1)}, bf16[1,257,192]{2,1,0:T(8,128)(2,1)S(1)}, u32[]{:S(2)}, u32[]{:S(2)}) %collective-permute-start) | collective-permute-done | bytes 98720 | tf_op jit(solution)/shard_map/ppermute | solution.py:11
  71.8 1.0 fusion.14
  72.8 1.3 collective-permute-start.1
  74.1 0.2 slice.160
  74.4 4.1 %collective-permute-done.1 = f32[8,1,192]{2,1,0:T(1,128)S(1)} collective-permute-done((f32[8,1,192]{2,1,0:T(1,128)S(1)}, f32[8,1,192]{2,1,0:T(1,128)S(1)}, u32[]{:S(2)}, u32[]{:S(2)}) %collective-permute-start.1) | collective-permute-done | bytes 6176 | tf_op jit(solution)/shard_map/ppermute | solution.py:11
  78.5 1.3 copy.88
  79.8 115.7 %all-reduce.5.cloned.1.call-done = (f32[576,192]{0,1:T(8,128)}, f32[576,192]{0,1:T(8,128)}, f32[576,192]{0,1:T(8,128)}) async-done(((f32[576,192]{0,1:T(8,128)}, f32[576,192]{0,1:T(8,128)}, f32[576,192]{0,1:T(8,128)}), (f32[576,192]{0,1:T(8,128)}, f32[576,192]{0,1:T(8,128)}, f32[576,192]{0,1:T(8,128)})) %all-reduce.5.cloned.1.call-update) | async-done | bytes 1327120 | tf_op jit(solution)/shard_map/psum | solution.py:74
  195.5 1.6 concatenate.15
  197.2 1.2 broadcast_multiply_fusion
  198.4 3.1 %copy.87 = f32[1728,192]{1,0:T(8,128)} copy(f32[1728,192]{0,1:T(8,128)} %broadcast_multiply_fusion) | data formatting | bytes 2654208 | tf_op jit(solution)/shard_map/mul | solution.py:76
  (22 shorter events, 0.4 us)
Async XLA Ops:
  7.2 14.9 %copy-start = (bf16[3,3,192,192]{3,2,1,0:T(8,128)(2,1)S(1)}, bf16[3,3,192,192]{3,2,1,0:T(8,128)(2,1)}, u32[]{:S(2)}) copy-start(bf16[3,3,192,192]{3,2,1,0:T(8,128)(2,1)} %param.9) | copy-start | bytes 1990660
  7.2 188.3 %all-reduce.5.cloned.1.call-start = ((), (), s32[]{:S(2)}) async-start(), calls=%async_computation | async-start | bytes 2949120 | tf_op jit(solution)/shard_map/psum | solution.py:74
  8.2 17.2 %collective-permute-start.2 = (bf16[1,256,192]{1,2,0:T(8,128)(2,1)S(1)}, bf16[1,256,192]{1,2,0:T(8,128)(2,1)S(1)}, u32[]{:S(2)}, u32[]{:S(2)}) collective-permute-start(bf16[1,256,192]{1,2,0:T(8,128)(2,1)S(1)} %slice.137), channel_id=1, source_target_pairs={{0,4},{4,8},{8,12},{12,16},{16,20},{20,24},{24,28},{1,5},{5,9},{9,... | collective-permute-start | bytes 294920 | tf_op jit(solution)/shard_map/ppermute | solution.py:11
  24.1 1.3 copy-start.4
  25.7 3.7 %collective-permute-start.3 = (bf16[9,1,192]{1,2,0:T(8,128)(2,1)S(1)}, bf16[9,1,192]{1,2,0:T(8,128)(2,1)S(1)}, u32[]{:S(2)}, u32[]{:S(2)}) collective-permute-start(bf16[9,1,192]{1,2,0:T(8,128)(2,1)S(1)} %slice.163), channel_id=1, source_target_pairs={{0,1},{1,2},{2,3},{4,5},{5,6},{6,7},{8,9},{9,10},{10,11},{12,13},{... | collective-permute-start | bytes 10376 | tf_op jit(solution)/shard_map/ppermute | solution.py:11
  44.4 5.0 %copy-start.3 = (bf16[4,1,128,1,192]{4,3,2,1,0:T(2,128)(2,1)S(1)}, bf16[4,1,128,1,192]{4,3,2,1,0:T(2,128)(2,1)}, u32[]{:S(2)}) copy-start(bf16[4,1,128,1,192]{4,3,2,1,0:T(2,128)(2,1)} %get-tuple-element.50) | copy-start | bytes 589828
  51.4 2.8 %copy-start.2 = (bf16[4,1,128,1,192]{4,3,2,1,0:T(2,128)(2,1)S(1)}, bf16[4,1,128,1,192]{4,3,2,1,0:T(2,128)(2,1)}, u32[]{:S(2)}) copy-start(bf16[4,1,128,1,192]{4,3,2,1,0:T(2,128)(2,1)} %get-tuple-element.46) | copy-start | bytes 589828
  55.4 1.7 copy-start.1
  63.9 7.9 %collective-permute-start = (bf16[1,257,192]{2,1,0:T(8,128)(2,1)S(1)}, bf16[1,257,192]{2,1,0:T(8,128)(2,1)S(1)}, u32[]{:S(2)}, u32[]{:S(2)}) collective-permute-start(bf16[1,257,192]{2,1,0:T(8,128)(2,1)S(1)} %slice.187), channel_id=1, source_target_pairs={{4,0},{8,4},{12,8},{16,12},{20,16},{24,20},{28,24},{5,1},{9,5},{13... | collective-permute-start | bytes 296072 | tf_op jit(solution)/shard_map/ppermute | solution.py:11
  72.8 5.6 %collective-permute-start.1 = (f32[8,1,192]{2,1,0:T(1,128)S(1)}, f32[8,1,192]{2,1,0:T(1,128)S(1)}, u32[]{:S(2)}, u32[]{:S(2)}) collective-permute-start(f32[8,1,192]{2,1,0:T(1,128)S(1)} %slice.162), channel_id=1, source_target_pairs={{1,0},{2,1},{3,2},{5,4},{6,5},{7,6},{9,8},{10,9},{11,10},{13,12},{... | collective-permute-start | bytes 18440 | tf_op jit(solution)/shard_map/ppermute | solution.py:11
Sparse Core Ops, SparseCore 0:
  57.2 138.2 all-reduce.4
where the time goes:
time: 209 us; the launch traced here: 208 us
  waiting for transfers between devices  125 us (60%)
  local copies, waits for them, and re-layouts  36.9 us (18%)
  between operations  14.3 us (7%)
  starting transfers between devices  9.95 us (5%)
  other arithmetic  8.95 us (4%)
  blocking collectives  8.84 us (4%)
  matrix products  4.68 us (2%)
    psum x1, waiting for transfers between devices, per_device(): buckets.append(lax.psum(terms, ('rows', 'cols')))  116 us
    slice x10, local copies, waits for them, and re-layouts, filter_terms(): split[start_row:start_row + count_rows, parity_row, start_col:start_col +...  13.3 us
    ppermute x4, starting transfers between devices, shifted(): return lax.ppermute(x, axis, pairs)  9.91 us
    ppermute x4, waiting for transfers between devices, shifted(): return lax.ppermute(x, axis, pairs)  8.96 us
    all_gather x1, blocking collectives, per_device(): whole = lax.all_gather(grad_out, 'cols', axis=0, tiled=True)  8.84 us
  transfers between devices with their start and end apart: 5, of which 3 were waited for; matrix products, arithmetic and copies ran while one was open for 8% of the time, Pallas kernels for 0%

commit v1 on v0

--- a/solution.py
+++ b/solution.py
@@ -71,7 +71,7 @@
     buckets = []
     for row_tap in range(3):
         terms = filter_terms(input_band, out_grad, (row_tap,))
-        buckets.append(lax.psum(terms, ("rows", "cols")))
+        buckets.append(jnp.sum(lax.all_gather(terms, ("rows", "cols")), axis=0))
     summed = jnp.concatenate(buckets, axis=0)
     filter_grad = summed.reshape(3, 3, chans, chans) * scale
     framed = jnp.pad(out_grad, ((1, 1), (1, 1), (0, 0)))

time: 209 us -> 403 us (1.93)
  waiting for transfers between devices: 125 us -> 303 us
  other arithmetic: 8.95 us -> 26.3 us
    all_gather x0 -> x3, waiting for transfers between devices: none -> 294 us  [per_device(): buckets.append(jnp.sum(lax.all_gather(terms, ('rows', 'cols')), axis=0))]
    psum x1 -> x0, waiting for transfers between devices: 116 us -> none  [per_device(): buckets.append(lax.psum(terms, ('rows', 'cols')))]
    reduce_sum x0 -> x3, other arithmetic: none -> 19 us  [per_device(): buckets.append(jnp.sum(lax.all_gather(terms, ('rows', 'cols')), axis=0))]
  transfers between devices with their start and end apart: 5 -> 7, of which waited for: 3 -> 6; matrix products, arithmetic and copies ran while one was open for 8% -> 8% of each run, Pallas kernels for 0% -> 0%
where the time goes in v1:
time: 403 us; the launch traced here: 402 us
  waiting for transfers between devices  303 us (75%)
  local copies, waits for them, and re-layouts  34.3 us (9%)
  other arithmetic  26.3 us (7%)
  between operations  14.1 us (3%)
  starting transfers between devices  10.8 us (3%)
  blocking collectives  8.84 us (2%)
  matrix products  4.66 us (1%)
    all_gather x3, waiting for transfers between devices, per_device(): buckets.append(jnp.sum(lax.all_gather(terms, ('rows', 'cols')), axis=0))  294 us
    reduce_sum x3, other arithmetic, per_device(): buckets.append(jnp.sum(lax.all_gather(terms, ('rows', 'cols')), axis=0))  19 us
    slice x10, local copies, waits for them, and re-layouts, filter_terms(): split[start_row:start_row + count_rows, parity_row, start_col:start_col +...  11.8 us
    ppermute x4, starting transfers between devices, shifted(): return lax.ppermute(x, axis, pairs)  10.5 us
    ppermute x4, waiting for transfers between devices, shifted(): return lax.ppermute(x, axis, pairs)  8.95 us
    all_gather x1, blocking collectives, per_device(): whole = lax.all_gather(grad_out, 'cols', axis=0, tiled=True)  8.84 us
  transfers between devices with their start and end apart: 7, of which 6 were waited for; matrix products, arithmetic and copies ran while one was open for 8% of the time, Pallas kernels for 0%

profile of v1, /device:TPU:0, one launch (start us, length us, event | category | flops | bytes accessed | tf_op | source)
XLA Modules:
  0.0 402.1 jit_solution(6410907812230691960)
XLA Ops:
  7.2 1.0 slice.137
  8.2 4.9 %collective-permute-start.2 = (bf16[1,256,192]{1,2,0:T(8,128)(2,1)S(1)}, bf16[1,256,192]{1,2,0:T(8,128)(2,1)S(1)}, u32[]{:S(2)}, u32[]{:S(2)}) collective-permute-start(bf16[1,256,192]{1,2,0:T(8,128)(2,1)S(1)} %slice.137), channel_id=1, source_target_pairs={{0,4},{4,8},{8,12},{12,16},{16,20},{20,24},{24,28},{1,5},{5,9},{9,... | collective-permute-start | bytes 294920 | tf_op jit(solution)/shard_map/ppermute | solution.py:11
  13.1 8.8 %all_gather.21 = bf16[4,512,192]{1,2,0:T(8,128)(2,1)S(1)} all-gather(bf16[1,512,192]{1,2,0:T(8,128)(2,1)} %param.7), channel_id=1, replica_groups=mesh['rows'=8,'cols'=4] {'cols'}, dimensions={0}, use_global_device_ids=true | all-gather | bytes 983040 | tf_op jit(solution)/shard_map/all_gather | solution.py:62
  21.9 1.2 constant_dynamic-update-slice_fusion
  23.3 3.0 collective-permute-start.3
  26.5 0.6 collective-permute-done.3
  27.1 2.7 pad_maximum_fusion.1
  29.8 2.1 copy.106
  31.9 1.3 pad.13.clone
  33.1 3.1 reshape.97
  36.3 4.4 %fusion.15 = (bf16[4,1,128,1,192]{4,3,2,1,0:T(2,128)(2,1)}, bf16[4,1,128,1,192]{4,3,2,1,0:T(2,128)(2,1)}, bf16[4,1,128,1,192]{4,3,2,1,0:T(2,128)(2,1)}, bf16[4,1...) fusion(bf16[5,2,129,2,192]{4,3,2,1,0:T(2,128)(2,1)S(1)} %reshape.97), kind=kLoop, calls=%fused_computation.36 | loop fusion | bytes 3538944 | tf_op jit(solution)/shard_map/slice | solution.py:44
  40.7 1.2 copy.97
  42.0 1.2 copy.99
  43.2 1.2 copy.98
  44.5 0.5 copy.100
  45.0 1.2 convolution_bitcast_fusion
  46.3 1.2 copy.95
  47.5 1.0 copy.94
  48.8 1.1 pad_maximum_fusion.3
  49.9 0.5 copy.96
  50.4 1.2 convolution_bitcast_fusion.1
  51.8 0.4 copy.91
  52.1 0.4 copy.90
  52.5 0.4 copy.89
  52.9 0.5 copy.92
  53.4 1.2 convolution_bitcast_fusion.2
  54.6 1.2 fusion.1
  55.8 0.4 slice_bitcast_fusion
  56.2 0.4 fusion.13
  57.1 1.4 copy.87
  58.5 2.9 reshape.96
  61.4 1.0 slice.187
  62.4 1.3 collective-permute-start
  63.7 1.8 slice.157
  65.5 3.8 collective-permute-done
  69.3 1.0 fusion.11
  70.3 1.3 collective-permute-start.1
  71.9 4.5 %collective-permute-done.1 = f32[8,1,192]{2,1,0:T(1,128)S(1)} collective-permute-done((f32[8,1,192]{2,1,0:T(1,128)S(1)}, f32[8,1,192]{2,1,0:T(1,128)S(1)}, u32[]{:S(2)}, u32[]{:S(2)}) %collective-permute-start.1) | collective-permute-done | bytes 6176 | tf_op jit(solution)/shard_map/ppermute | solution.py:11
  76.5 1.3 copy.102
  77.7 84.7 %all-gather.14.cloned.1.call-done = f32[32,576,192]{1,2,0:T(8,128)} async-done(((f32[1,576,192]{1,2,0:T(8,128)}), f32[32,576,192]{1,2,0:T(8,128)}) %all-gather.14.cloned.1.call-update) | async-done | bytes 14155792 | tf_op jit(solution)/shard_map/all_gather | solution.py:74
  162.4 6.3 %reduce_sum.29 = f32[576,192]{0,1:T(8,128)S(1)} reduce(f32[32,576,192]{1,2,0:T(8,128)} %all-gather.14.cloned.1.call-done, f32[]{:T(128)} %constant.70.clone.1), dimensions={0}, to_apply=%region_2.3 | reduce | flops 3428352 | bytes 14598148 | tf_op jit(solution)/shard_map/reduce_sum | solution.py:74
  168.7 104.4 %all-gather.12.cloned.1.call-done = f32[32,576,192]{1,2,0:T(8,128)} async-done(((f32[1,576,192]{1,2,0:T(8,128)}), f32[32,576,192]{1,2,0:T(8,128)}) %all-gather.12.cloned.1.call-update) | async-done | bytes 14155792 | tf_op jit(solution)/shard_map/all_gather | solution.py:74
  273.2 6.3 %reduce_sum.28 = f32[576,192]{0,1:T(8,128)S(1)} reduce(f32[32,576,192]{1,2,0:T(8,128)} %all-gather.12.cloned.1.call-done, f32[]{:T(128)} %constant.70.clone.1), dimensions={0}, to_apply=%region_1.2 | reduce | flops 3428352 | bytes 14598148 | tf_op jit(solution)/shard_map/reduce_sum | solution.py:74
  279.5 105.0 %all-gather.10.cloned.1.call-done = f32[32,576,192]{1,2,0:T(8,128)} async-done(((f32[1,576,192]{1,2,0:T(8,128)}), f32[32,576,192]{1,2,0:T(8,128)}) %all-gather.10.cloned.1.call-update) | async-done | bytes 14155792 | tf_op jit(solution)/shard_map/all_gather | solution.py:74
  384.5 6.3 %reduce_sum.27 = f32[576,192]{0,1:T(8,128)S(1)} reduce(f32[32,576,192]{1,2,0:T(8,128)} %all-gather.10.cloned.1.call-done, f32[]{:T(128)} %constant.70.clone.1), dimensions={0}, to_apply=%region_0.1 | reduce | flops 3428352 | bytes 14598148 | tf_op jit(solution)/shard_map/reduce_sum | solution.py:74
  390.8 0.5 concatenate.15
  391.3 1.2 broadcast_multiply_fusion
  392.5 3.1 copy.101
  (31 shorter events, 2.0 us)
Async XLA Ops:
  7.2 47.4 %copy-start = (bf16[3,3,192,192]{3,2,1,0:T(8,128)(2,1)S(1)}, bf16[3,3,192,192]{3,2,1,0:T(8,128)(2,1)}, u32[]{:S(2)}) copy-start(bf16[3,3,192,192]{3,2,1,0:T(8,128)(2,1)} %param.9) | copy-start | bytes 1990660
  7.2 155.2 %all-gather.14.cloned.1.call-start = ((), (), s32[]{:S(2)}) async-start(), calls=%async_computation.2 | async-start | bytes 16220160 | tf_op jit(solution)/shard_map/all_gather | solution.py:74
  8.2 13.7 %collective-permute-start.2 = (bf16[1,256,192]{1,2,0:T(8,128)(2,1)S(1)}, bf16[1,256,192]{1,2,0:T(8,128)(2,1)S(1)}, u32[]{:S(2)}, u32[]{:S(2)}) collective-permute-start(bf16[1,256,192]{1,2,0:T(8,128)(2,1)S(1)} %slice.137), channel_id=1, source_target_pairs={{0,4},{4,8},{8,12},{12,16},{16,20},{20,24},{24,28},{1,5},{5,9},{9,... | collective-permute-start | bytes 294920 | tf_op jit(solution)/shard_map/ppermute | solution.py:11
  23.3 3.8 collective-permute-start.3
  44.5 3.0 copy-start.4
  44.5 3.9 copy-start.3
  46.2 227.0 %all-gather.12.cloned.1.call-start = ((), (), s32[]{:S(2)}) async-start(), calls=%async_computation.1 | async-start | bytes 16220160 | tf_op jit(solution)/shard_map/all_gather | solution.py:74
  48.8 3.0 copy-start.2
  51.5 332.9 %all-gather.10.cloned.1.call-start = ((), (), s32[]{:S(2)}) async-start(), calls=%async_computation | async-start | bytes 16220160 | tf_op jit(solution)/shard_map/all_gather | solution.py:74
  62.4 6.9 %collective-permute-start = (bf16[1,257,192]{2,1,0:T(8,128)(2,1)S(1)}, bf16[1,257,192]{2,1,0:T(8,128)(2,1)S(1)}, u32[]{:S(2)}, u32[]{:S(2)}) collective-permute-start(bf16[1,257,192]{2,1,0:T(8,128)(2,1)S(1)} %slice.187), channel_id=1, source_target_pairs={{4,0},{8,4},{12,8},{16,12},{20,16},{24,20},{28,24},{5,1},{9,5},{13... | collective-permute-start | bytes 296072 | tf_op jit(solution)/shard_map/ppermute | solution.py:11
  70.3 6.1 %collective-permute-start.1 = (f32[8,1,192]{2,1,0:T(1,128)S(1)}, f32[8,1,192]{2,1,0:T(1,128)S(1)}, u32[]{:S(2)}, u32[]{:S(2)}) collective-permute-start(f32[8,1,192]{2,1,0:T(1,128)S(1)} %slice.162), channel_id=1, source_target_pairs={{1,0},{2,1},{3,2},{5,4},{6,5},{7,6},{9,8},{10,9},{11,10},{13,12},{... | collective-permute-start | bytes 18440 | tf_op jit(solution)/shard_map/ppermute | solution.py:11
  391.3 4.3 %copy-start.1 = (bf16[3,3,192,192]{3,2,1,0:T(8,128)(2,1)S(1)}, bf16[3,3,192,192]{3,2,1,0:T(8,128)(2,1)}, u32[]{:S(2)}) copy-start(bf16[3,3,192,192]{3,2,1,0:T(8,128)(2,1)} %param.9) | copy-start | bytes 1990660
Sparse Core Ops, SparseCore 0:
  46.3 116.0 all-gather.13
  165.3 107.7 all-gather.11
  276.7 107.7 all-gather.9
